TPU v7x, 256 devices: a 2x2x32 block of a 4x8x32 slice. The times are simulated.
256 devices in a mesh: groups: 4 (over y, x), mp: 64 (over z, core).
Axes of the slice: x: 2, y: 2, z: 32, core: 2. Of those that a mesh axis runs over, the one named last changes fastest.
The devices are a block of a 4x8x32 slice.
Arguments:
- hidden: bfloat16 [2048, 4096], P(('groups', 'mp')), parts along dimension 0, may hold values from -6 to 6
- norm_gain_attn: float32 [4096], replicated, may hold values from 0.5 to 1.5
- w_query: bfloat16 [4096, 4096], P(None, 'mp'), may hold values from -0.09375 to 0.09375
- entering_kv: bfloat16 [32, 2048, 8192], P('groups', 'mp'), parts along dimension 0, may hold values from -60 to 60
- cached_kv: bfloat16 [32, 2048, 8192], P('groups', None, 'mp'), parts along dimension 0, may hold values from -60 to 60
- enc_lengths: int32 [2, 32], P(None, 'groups'), parts along dimension 1, may hold values from 128 to 2048
- w_out: bfloat16 [4096, 4096], P('mp'), may hold values from -0.09375 to 0.09375
- norm_gain_ffn: float32 [4096], replicated, may hold values from 0.5 to 1.5
- w_gate: bfloat16 [4096, 10240], P(None, 'mp'), may hold values from -0.09375 to 0.09375
- w_up: bfloat16 [4096, 10240], P(None, 'mp'), may hold values from -0.09375 to 0.09375
- w_down: bfloat16 [10240, 4096], P('mp'), may hold values from -0.0625 to 0.0625
Outputs:
- output: bfloat16 [2048, 4096], P(('groups', 'mp')), parts along dimension 0
There are 4 independent parts, one for each index of `groups`. A program takes and returns all parts, laid end to end along the dimension named above; an argument that names none is the same for every part. Nothing has to cross between parts.
All inputs are finite; a program needn't handle non-finite values.
Results may differ from a plain program's by a relative error of at most 0.0095.
The roundings to bfloat16 on the way count: a program that leaves them out, or rounds other values in their place, can miss the bound.
Values may be sent and summed in bfloat16 or wider, within the bound.
No kernel may reach another device: no remote copies, remote signals or barrier semaphores. Data moves between devices by JAX's collectives and lax.ppermute only.
A program may use at most 128 MiB of HBM per device.

v0:
```python
import jax
import jax.numpy as jnp
from jax import lax
from jax.sharding import Mesh
from jax.sharding import PartitionSpec as P

DH = 64
S = 2048
QLEN = 32
MP = ("mp_0", "mp_1")
GROUPS_MP = ("groups", "mp_0", "mp_1")


epsilon = 0.1


def joined_along(parts, dim):
    shape = list(parts.shape[1:])
    shape[dim] *= parts.shape[0]
    return jnp.moveaxis(parts, 0, dim).reshape(shape)


def all_blocks(x, axes, turns):
    parts = x[None]
    for k in turns:
        parts = lax.all_gather(parts, axes[k], axis=0, tiled=True)
    block = [lax.axis_size(axes[k]) for k in reversed(turns)]
    parts = parts.reshape(*block, *x.shape)
    turned = sorted(range(len(turns)), key=lambda place: turns[len(turns) - 1 - place])
    return parts.transpose(*turned, *range(len(turns), parts.ndim)).reshape(-1, *x.shape)


def gather_axes(x, axes, turns, dim):
    return joined_along(all_blocks(x, axes, turns), dim)


def sum_in_order(parts, axes, turns):
    inside = parts.shape[1:]
    parts = parts.reshape(*(lax.axis_size(a) for a in axes), *inside)
    parts = jnp.moveaxis(parts, turns, range(len(axes))).reshape(-1, *inside)
    for k in turns:
        parts = lax.psum_scatter(parts, axes[k], scatter_dimension=0, tiled=True)
    return parts[0]


def in_blocks(x, dim, size):
    before, after = (x.shape[:dim], x.shape[dim + 1 :])
    return jnp.moveaxis(x.reshape(*before, size, -1, *after), dim, 0)


def sum_by_axis(x, axes, turns, dim):
    size = lax.axis_size(axes)
    return sum_in_order(in_blocks(x, dim, size), axes, turns)


def normalize(matrix, gain_row):
    values = matrix.astype(jnp.float32)
    mean_square = jnp.mean(values * values, axis=-1, keepdims=True)
    return (values * lax.rsqrt(mean_square + epsilon) * gain_row).astype(jnp.bfloat16)


def attend(query, key_value, lengths):
    requests = lengths.shape[0]
    head_count = key_value.shape[2] // (2 * DH)
    query_heads = query.reshape(requests, QLEN, head_count, DH)
    paired = key_value.reshape(requests, S, head_count, 2, DH)
    key_part = paired[:, :, :, 0, :]
    value_part = paired[:, :, :, 1, :]
    scores = jnp.einsum(
        "rqhd,rshd->rhqs", query_heads, key_part, preferred_element_type=jnp.float32
    )
    usable = (jnp.arange(S, dtype=jnp.int32)[None, :] < lengths[:, None])[:, None, None, :]
    masked = jnp.where(usable, scores, -1e30)
    largest = jnp.max(masked, axis=-1, keepdims=True)
    exponent = jnp.where(usable, jnp.exp(masked - largest), 0.0)
    weights = (exponent / jnp.sum(exponent, axis=-1, keepdims=True)).astype(jnp.bfloat16)
    context = jnp.einsum("rhqs,rshd->rqhd", weights, value_part, preferred_element_type=jnp.float32)
    return context.astype(jnp.bfloat16).reshape(requests * QLEN, head_count * DH)


def per_device(
    hidden,
    norm_gain_attn,
    w_query,
    entering_kv,
    cached_kv,
    enc_lengths,
    w_out,
    norm_gain_ffn,
    w_gate,
    w_up,
    w_down,
):
    arrived = lax.all_to_all(entering_kv, MP, split_axis=2, concat_axis=1, tiled=True)
    query = jnp.dot(
        gather_axes(normalize(hidden, norm_gain_attn), MP, (0, 1), 0),
        w_query,
        preferred_element_type=jnp.float32,
    ).astype(jnp.bfloat16)
    split_row = query.shape[0] // 2
    context = jnp.concatenate(
        [
            attend(query[:split_row], arrived, enc_lengths[0]),
            attend(query[split_row:], cached_kv, enc_lengths[1]),
        ],
        axis=0,
    )
    attention = sum_by_axis(
        jnp.dot(context, w_out, preferred_element_type=jnp.float32), MP, (1, 0), 0
    )
    residual = (hidden.astype(jnp.float32) + attention).astype(jnp.bfloat16)
    portion = lax.all_gather(normalize(residual, norm_gain_ffn), MP, axis=0, tiled=True)
    gate = jnp.dot(portion, w_gate, preferred_element_type=jnp.float32)
    upward = jnp.dot(portion, w_up, preferred_element_type=jnp.float32)
    activated = (jax.nn.gelu(gate, approximate=True) * upward).astype(jnp.bfloat16)
    feed_out = sum_by_axis(
        jnp.dot(activated, w_down, preferred_element_type=jnp.float32), MP, (1, 0), 0
    )
    return (residual.astype(jnp.float32) + feed_out).astype(jnp.bfloat16)


def solution(mesh):
    torus = Mesh(mesh.devices.reshape(mesh.shape["groups"], 32, 2), ("groups", "mp_0", "mp_1"))
    in_specs = (
        P(GROUPS_MP, None),
        P(),
        P(None, MP),
        P("groups", MP, None),
        P("groups", None, MP),
        P(None, "groups"),
        P(MP, None),
        P(),
        P(None, MP),
        P(None, MP),
        P(MP, None),
    )
    out_specs = P(GROUPS_MP, None)
    return jax.shard_map(
        per_device, mesh=torus, in_specs=in_specs, out_specs=out_specs, check_vma=False
    )
```

profile of v0, /device:TPU:38, one launch (start us, length us, event | category | flops | bytes accessed | tf_op | source)
XLA Modules:
  0.0 1091.6 jit_solution(3364855448065217536)
XLA Ops:
  6.5 0.0 copy-start
  6.6 17.0 %copy.39 = bf16[8,32,8192]{1,0,2:T(8,128)(2,1)} copy(bf16[8,32,8192]{2,1,0:T(8,128)(2,1)} %param.14) | data formatting | bytes 8388608 | tf_op args[3]
  23.5 25.0 %reshape.166 = bf16[64,2,16384]{2,1,0:T(2,128)(2,1)} reshape(bf16[8192,8,32]{2,1,0:T(8,128)(2,1)} %bitcast.80) | data formatting | bytes 8388608
  48.6 0.0 copy-start.2
  48.6 0.0 copy-start.5
  48.6 34.4 %all-to-all-start = ((bf16[64,2,16384]{2,1,0:T(2,128)(2,1)}), bf16[64,2,16384]{2,1,0:T(2,128)(2,1)}, u32[]{:S(2)}, u32[]{:S(2)}) async-start(bf16[64,2,16384]{2,1,0:T(2,128)(2,1)} %reshape.166), calls=%async_computation | async-start | bytes 8388608 | tf_op jit(solution)/shard_map/all_to_all | solution.py:94
  83.0 0.1 all-gather.9.cloned.1.call-start
  83.1 0.0 copy-done.2
  83.1 0.1 fusion.32
  83.2 0.0 copy-done.5
  83.2 0.7 fusion.34
  83.9 0.1 all-gather.9.cloned.1.call-update
  84.0 0.1 all-gather.5.cloned.1.call-start
  84.1 284.8 %all-gather.9.cloned.1.call-done = bf16[256,4096]{1,0:T(8,128)(2,1)} async-done(((bf16[8,4096]{1,0:T(8,128)(2,1)}), bf16[256,4096]{1,0:T(8,128)(2,1)}) %all-gather.9.cloned.1.call-update) | async-done | bytes 2097168 | tf_op jit(solution)/shard_map/all_gather | solution.py:26
  368.8 0.1 all-gather.5.cloned.1.call-update
  368.9 0.0 copy-start.7
  368.9 0.2 reduce-scatter.5.cloned.1.call-start
  369.2 6.6 copy.44
  375.7 0.0 copy-done.7
  375.7 0.1 iota_compare_fusion
  375.8 25.7 %all-gather.5.cloned.1.call-done = bf16[64,8,4096]{2,1,0:T(8,128)(2,1)} async-done(((bf16[32,8,4096]{2,1,0:T(8,128)(2,1)}), bf16[64,8,4096]{2,1,0:T(8,128)(2,1)}) %all-gather.5.cloned.1.call-update) | async-done | bytes 4194320 | tf_op jit(solution)/shard_map/all_gather | solution.py:26
  401.5 2.5 copy.37
  404.0 0.0 copy-done.3
  404.0 1.4 convolution_convert_fusion
  405.5 0.7 copy.38
  406.2 0.1 copy.43
  406.3 3.8 fusion.52
  410.1 3.0 fusion.17
  413.1 70.5 %all-to-all-done = bf16[64,2,16384]{2,1,0:T(2,128)(2,1)} async-done(((bf16[64,2,16384]{2,1,0:T(2,128)(2,1)}), bf16[64,2,16384]{2,1,0:T(2,128)(2,1)}, u32[]{:S(2)}, u32[]{:S(2)}) %all-to-all-start) | async-done | bytes 4194336 | tf_op jit(solution)/shard_map/all_to_all | solution.py:94
  483.6 21.9 %reshape.167 = bf16[8192,8,32]{2,1,0:T(8,128)(2,1)} reshape(bf16[64,2,16384]{2,1,0:T(2,128)(2,1)} %all-to-all-done) | data formatting | bytes 8388608
  505.5 17.5 %copy.40 = bf16[8,32,64,128]{3,1,2,0:T(8,128)(2,1)} copy(bf16[8,32,64,128]{1,0,3,2:T(8,128)(2,1)} %bitcast.79) | data formatting | bytes 8388608 | tf_op jit(solution)/shard_map/all_to_all | solution.py:94
  523.0 14.7 %reshape.154 = bf16[8,2048,1,2,64]{4,3,1,0,2:T(2,128)(2,1)} reshape(bf16[8,64,32,128]{3,2,1,0:T(8,128)(2,1)} %bitcast.85) | data formatting | bytes 8388608 | tf_op jit(solution)/shard_map/reshape | solution.py:66
  537.7 17.8 %fusion.50 = (bf16[8,2048,1,1,64]{4,3,1,0,2:T(2,128)(2,1)}, bf16[8,2048,1,1,64]{4,3,1,0,2:T(2,128)(2,1)}) fusion(bf16[8,2048,1,2,64]{4,3,1,0,2:T(2,128)(2,1)} %reshape.154), kind=kLoop, calls=%fused_computation.67 | loop fusion | bytes 8388608 | tf_op jit(solution)/shard_map/slice | solution.py:67
  555.5 17.5 %copy.49 = bf16[8,2048,1,1,64]{1,4,0,3,2:T(8,128)(2,1)S(1)} copy(bf16[8,2048,1,1,64]{4,3,1,0,2:T(2,128)(2,1)} %get-tuple-element.7) | data formatting | bytes 4194304
  573.0 19.4 %copy.50 = bf16[8,2048,1,1,64]{1,4,0,3,2:T(8,128)(2,1)} copy(bf16[8,2048,1,1,64]{4,3,1,0,2:T(2,128)(2,1)} %get-tuple-element.8) | data formatting | bytes 4194304
  592.4 3.6 fusion.53
  596.0 3.0 fusion.14
  599.0 0.0 copy-done.4
  599.1 1.2 fusion.40
  600.3 3.8 copy.47
  604.1 0.1 reduce-scatter.5.cloned.1.call-update
  604.1 0.1 reduce-scatter.7.cloned.1.call-start
  604.2 15.8 %reduce-scatter.5.cloned.1.call-done = f32[32,8,4096]{2,1,0:T(8,128)} async-done(((f32[64,8,4096]{2,1,0:T(8,128)}), f32[32,8,4096]{2,1,0:T(8,128)}) %reduce-scatter.5.cloned.1.call-update) | async-done | bytes 4194320 | tf_op jit(solution)/shard_map/reduce_scatter | solution.py:42
  620.0 0.1 reduce-scatter.7.cloned.1.call-update
  620.0 0.1 all-gather.7.cloned.1.call-start
  620.1 142.6 %reduce-scatter.7.cloned.1.call-done = f32[1,8,4096]{2,1,0:T(8,128)} async-done(((f32[32,8,4096]{2,1,0:T(8,128)}), f32[1,8,4096]{2,1,0:T(8,128)}) %reduce-scatter.7.cloned.1.call-update) | async-done | bytes 131088 | tf_op jit(solution)/shard_map/reduce_scatter | solution.py:42
  762.7 1.1 fusion.36
  763.7 0.0 copy-done.6
  763.7 0.7 fusion.38
  764.4 0.1 all-gather.7.cloned.1.call-update
  764.5 0.0 copy-start.1
  764.5 0.3 reduce-scatter.9.cloned.1.call-start
  764.8 130.4 %all-gather.7.cloned.1.call-done = bf16[512,4096]{1,0:T(8,128)(2,1)} async-done(((bf16[8,4096]{1,0:T(8,128)(2,1)}), bf16[512,4096]{1,0:T(8,128)(2,1)}) %all-gather.7.cloned.1.call-update) | async-done | bytes 4194320 | tf_op jit(solution)/shard_map/all_gather | solution.py:112
  895.2 4.1 fusion.56
  899.4 0.0 copy-done
  899.4 0.0 copy-done.1
  899.4 8.3 fusion.13
  907.7 7.6 copy.48
  915.3 0.1 reduce-scatter.9.cloned.1.call-update
  915.3 0.1 reduce-scatter.11.cloned.1.call-start
  915.4 25.0 %reduce-scatter.9.cloned.1.call-done = f32[32,8,4096]{2,1,0:T(8,128)} async-done(((f32[64,8,4096]{2,1,0:T(8,128)}), f32[32,8,4096]{2,1,0:T(8,128)}) %reduce-scatter.9.cloned.1.call-update) | async-done | bytes 4194320 | tf_op jit(solution)/shard_map/reduce_scatter | solution.py:42
  940.4 0.1 reduce-scatter.11.cloned.1.call-update
  940.5 142.7 %reduce-scatter.11.cloned.1.call-done = f32[1,8,4096]{2,1,0:T(8,128)} async-done(((f32[32,8,4096]{2,1,0:T(8,128)}), f32[1,8,4096]{2,1,0:T(8,128)}) %reduce-scatter.11.cloned.1.call-update) | async-done | bytes 131088 | tf_op jit(solution)/shard_map/reduce_scatter | solution.py:42
  1083.2 1.5 fusion.39
  (7 shorter events, 0.0 us)
Async XLA Ops:
  6.5 892.8 %copy-start = (bf16[160,4096]{1,0:T(8,128)(2,1)S(1)}, bf16[160,4096]{1,0:T(8,128)(2,1)}, u32[]{:S(2)}) copy-start(bf16[160,4096]{1,0:T(8,128)(2,1)} %param.21) | copy-start | bytes 3932164
  48.6 34.5 %copy-start.2 = (bf16[8,4096]{1,0:T(8,128)(2,1)S(1)}, bf16[8,4096]{1,0:T(8,128)(2,1)}, u32[]{:S(2)}) copy-start(bf16[8,4096]{1,0:T(8,128)(2,1)} %param.11) | copy-start | bytes 196612
  48.6 34.6 %copy-start.5 = (f32[4096]{0:T(1024)S(1)}, f32[4096]{0:T(1024)}, u32[]{:S(2)}) copy-start(f32[4096]{0:T(1024)} %param.12) | copy-start | bytes 49156
  48.6 435.0 %all-to-all-start = ((bf16[64,2,16384]{2,1,0:T(2,128)(2,1)}), bf16[64,2,16384]{2,1,0:T(2,128)(2,1)}, u32[]{:S(2)}, u32[]{:S(2)}) async-start(bf16[64,2,16384]{2,1,0:T(2,128)(2,1)} %reshape.166), calls=%async_computation | async-start | bytes 8388608 | tf_op jit(solution)/shard_map/all_to_all | solution.py:94
  83.0 285.9 %all-gather.9.cloned.1.call-start = ((), (), s32[]{:S(2)}) async-start(), calls=%async_computation.11 | async-start | bytes 2162688 | tf_op jit(solution)/shard_map/all_gather | solution.py:26
  84.0 317.5 %all-gather.5.cloned.1.call-start = ((), (), s32[]{:S(2)}) async-start(), calls=%async_computation.5 | async-start | bytes 6291456 | tf_op jit(solution)/shard_map/all_gather | solution.py:26
  368.9 6.8 copy-start.7
  368.9 251.0 %reduce-scatter.5.cloned.1.call-start = ((), (), s32[]{:S(2)}) async-start(), calls=%async_computation.6 | async-start | bytes 12582912 | tf_op jit(solution)/shard_map/reduce_scatter | solution.py:42
  401.5 2.5 copy-start.3
  596.0 3.1 copy-start.4
  604.1 158.5 %reduce-scatter.7.cloned.1.call-start = ((), (), s32[]{:S(2)}) async-start(), calls=%async_computation.7 | async-start | bytes 4325376 | tf_op jit(solution)/shard_map/reduce_scatter | solution.py:42
  620.0 143.8 %copy-start.6 = (f32[4096]{0:T(1024)S(1)}, f32[4096]{0:T(1024)}, u32[]{:S(2)}) copy-start(f32[4096]{0:T(1024)} %param.18) | copy-start | bytes 49156
  620.0 275.2 %all-gather.7.cloned.1.call-start = ((), (), s32[]{:S(2)}) async-start(), calls=%async_computation.8 | async-start | bytes 4259840 | tf_op jit(solution)/shard_map/all_gather | solution.py:112
  764.5 134.9 %copy-start.1 = (bf16[4096,160]{0,1:T(8,128)(2,1)S(1)}, bf16[4096,160]{0,1:T(8,128)(2,1)}, u32[]{:S(2)}) copy-start(bf16[4096,160]{0,1:T(8,128)(2,1)} %param.20) | copy-start | bytes 3932164
  764.5 175.9 %reduce-scatter.9.cloned.1.call-start = ((), (), s32[]{:S(2)}) async-start(), calls=%async_computation.9 | async-start | bytes 12582912 | tf_op jit(solution)/shard_map/reduce_scatter | solution.py:42
  915.3 167.9 %reduce-scatter.11.cloned.1.call-start = ((), (), s32[]{:S(2)}) async-start(), calls=%async_computation.10 | async-start | bytes 4325376 | tf_op jit(solution)/shard_map/reduce_scatter | solution.py:42
Sparse Core Ops, SparseCore 0:
  85.6 283.1 all-gather.8
  370.7 30.8 all-gather.4
  604.3 15.6 reduce-scatter.4
  622.4 140.2 reduce-scatter.6
  764.6 130.5 all-gather.6
  915.5 24.9 reduce-scatter.8
  943.0 140.1 reduce-scatter.10
where the time goes:
time: 1100 us; the launch traced here: 1090 us
  waiting for transfers between devices  838 us (76%)
  local copies, waits for them, and re-layouts  172 us (16%)
  starting transfers between devices  35.2 us (3%)
  matrix products  28.5 us (3%)
  between operations  13.6 us (1%)
    reduce_scatter x4, waiting for transfers between devices, sum_in_order(): parts = lax.psum_scatter(parts, axes[k], scatter_dimension=0, tiled=True)  326 us
    all_gather x2, waiting for transfers between devices, all_blocks(): parts = lax.all_gather(parts, axes[k], axis=0, tiled=True)  310 us
    all_gather x1, waiting for transfers between devices, per_device(): lax.all_gather(normalize(residual, norm_gain_ffn), MP, axis=0, tiled=True)  130 us
    unnamed x22, local copies, waits for them, and re-layouts  107 us
    all_to_all x1, waiting for transfers between devices, per_device(): lax.all_to_all(entering_kv, MP, split_axis=2, concat_axis=1, tiled=True)  70.5 us
    all_to_all x1, starting transfers between devices, per_device(): lax.all_to_all(entering_kv, MP, split_axis=2, concat_axis=1, tiled=True)  34.4 us
  transfers between devices with their start and end apart: 8, of which 8 were waited for; matrix products, arithmetic and copies ran while one was open for 2% of the time, Pallas kernels for 0%

commit v1 on v0

v1 whole, which is shorter than its diff:
```python
import jax
import jax.numpy as jnp
from jax import lax
from jax.experimental import pallas as pl
from jax.experimental.pallas import tpu as pltpu
from jax.sharding import Mesh
from jax.sharding import PartitionSpec as P

DH = 64
S = 2048
QLEN = 32
MP = ("mp_0", "mp_1")
GROUPS_MP = ("groups", "mp_0", "mp_1")
RING = 32
FAR = 8
NEG = -1e30
epsilon = 0.1

SLOTS = [(8 * k + (g if g < 5 else g - 8)) % RING for g in range(8) for k in range(4)]


def fetch(x, k):
    return lax.ppermute(x, "mp_0", [(i, (i - k) % RING) for i in range(RING)])


def other_core(x):
    return lax.ppermute(x, "mp_1", [(0, 1), (1, 0)])


def ring_gather(x):
    half = x.shape[1] // 2
    ahead = fetch(x, FAR)
    behind = fetch(x, -FAR)
    opposite = jnp.concatenate([fetch(ahead[:, :half], FAR), fetch(behind[:, half:], -FAR)], axis=1)
    here = jnp.stack([x, ahead, opposite, behind])
    right, left = [here], [here]
    for _ in range(3):
        right.append(fetch(right[-1], 1))
        left.append(fetch(left[-1], -1))
    right_last = fetch(right[3][:2], 1)
    left_last = fetch(jnp.concatenate([left[3][3:], left[3][:1]]), -1)
    return jnp.concatenate([*right, right_last, left_last, left[3], left[2], left[1]])


def ring_reduce(parts, join, finish, narrow):
    block = [parts[4 * g : 4 * g + 4] for g in range(8)]
    from_left = fetch(narrow(block[4][:2]), -1)
    from_right = fetch(narrow(block[4][2:]), 1)
    right = jnp.concatenate([join(block[3][:2], from_left), narrow(block[3][2:])])
    left = jnp.concatenate(
        [join(block[5][:1], from_right[1:]), narrow(block[5][1:3]), join(block[5][3:], from_right[:1])]
    )
    for step in (2, 1):
        right = join(block[step], fetch(right, -1))
        left = join(block[8 - step], fetch(left, 1))
    total = finish(block[0], fetch(right, -1), fetch(left, 1))
    half = total.shape[2] // 2
    ahead = fetch(narrow(total[2:3, :, :half]), -FAR)
    behind = fetch(narrow(total[2:3, :, half:]), FAR)
    to_ahead = jnp.concatenate(
        [join(total[1:2, :, :half], ahead), narrow(total[1:2, :, half:])], axis=2
    )
    to_behind = jnp.concatenate(
        [narrow(total[3:4, :, :half]), join(total[3:4, :, half:], behind)], axis=2
    )
    return total[0:1], fetch(to_ahead, -FAR), fetch(to_behind, FAR)


def narrow_sum(x):
    return x.astype(jnp.bfloat16)


def join_sum(mine, arrived):
    return (mine.astype(jnp.float32) + arrived.astype(jnp.float32)).astype(jnp.bfloat16)


def add_three(mine, one, two):
    return mine.astype(jnp.float32) + (one.astype(jnp.float32) + two.astype(jnp.float32))


def sum_over_ring(parts):
    return add_three(*ring_reduce(parts, join_sum, add_three, narrow_sum))[0]


def normalize(matrix, gain_row):
    values = matrix.astype(jnp.float32)
    mean_square = jnp.mean(values * values, axis=-1, keepdims=True)
    return (values * lax.rsqrt(mean_square + epsilon) * gain_row).astype(jnp.bfloat16)


def attend(query, key_value, lengths):
    requests = lengths.shape[0]
    head_count = key_value.shape[2] // (2 * DH)
    query_heads = query.reshape(requests, QLEN, head_count, DH)
    paired = key_value.reshape(requests, S, head_count, 2, DH)
    key_part = paired[:, :, :, 0, :]
    value_part = paired[:, :, :, 1, :]
    scores = jnp.einsum(
        "rqhd,rshd->rhqs", query_heads, key_part, preferred_element_type=jnp.float32
    )
    usable = (jnp.arange(S, dtype=jnp.int32)[None, :] < lengths[:, None])[:, None, None, :]
    masked = jnp.where(usable, scores, NEG)
    largest = jnp.max(masked, axis=-1, keepdims=True)
    exponent = jnp.where(usable, jnp.exp(masked - largest), 0.0)
    weights = (exponent / jnp.sum(exponent, axis=-1, keepdims=True)).astype(jnp.bfloat16)
    context = jnp.einsum("rhqs,rshd->rqhd", weights, value_part, preferred_element_type=jnp.float32)
    return context.astype(jnp.bfloat16).reshape(requests * QLEN, head_count * DH)


def every_second_head(key_value, parity):
    requests, positions, width = key_value.shape
    heads = width // (2 * 2 * DH)
    together = 4
    lane = 2 * DH

    def body(parity_ref, *refs):
        for j in range(together):
            refs[together][:, :, j * lane : (j + 1) * lane] = refs[j][...]

    def column(j):
        return lambda i, p: (0, 0, 2 * (together * i + j) + p[0])

    return pl.pallas_call(
        body,
        grid_spec=pltpu.PrefetchScalarGridSpec(
            num_scalar_prefetch=1,
            grid=(heads // together,),
            in_specs=[pl.BlockSpec((requests, positions, lane), column(j)) for j in range(together)],
            out_specs=pl.BlockSpec((requests, positions, together * lane), lambda i, p: (0, 0, i)),
        ),
        out_shape=jax.ShapeDtypeStruct((requests, positions, heads * lane), key_value.dtype),
        name="every_second_head",
    )(parity, *([key_value] * together))


def split_rows(value):
    high = value.astype(jnp.bfloat16)
    rest = value - high.astype(jnp.float32)
    middle = rest.astype(jnp.bfloat16)
    low = (rest - middle.astype(jnp.float32)).astype(jnp.bfloat16)
    return [high, middle, low]


def pack(sums, largest, weight):
    rows = split_rows(largest) + split_rows(weight)
    zero = jnp.zeros((10, sums.shape[1]), jnp.float32)
    tail = jnp.concatenate([r.astype(jnp.float32) for r in rows] + [zero], axis=0)
    return jnp.concatenate([sums.astype(jnp.bfloat16), tail.astype(jnp.bfloat16)], axis=0)


def unpack(part):
    sums = part[:DH].astype(jnp.float32)
    tail = part[DH:].astype(jnp.float32)
    return sums, tail[0:1] + tail[1:2] + tail[2:3], tail[3:4] + tail[4:5] + tail[5:6]


def merge(first, second):
    sums_a, largest_a, weight_a = first
    sums_b, largest_b, weight_b = second
    largest = jnp.maximum(largest_a, largest_b)
    scale_a = jnp.exp(largest_a - largest)
    scale_b = jnp.exp(largest_b - largest)
    return (
        sums_a * scale_a + sums_b * scale_b,
        largest,
        weight_a * scale_a + weight_b * scale_b,
    )


def partial_attention(query, own, partner, usable, columns):
    count, _, tokens = query.shape
    requests, positions, _ = own.shape
    lane = 2 * DH
    rows = requests * positions

    def body(columns_ref, q_ref, own_ref, partner_ref, usable_ref, out_ref):
        kv = jnp.concatenate(
            [own_ref[...].reshape(rows, lane), partner_ref[...].reshape(rows, lane)], axis=0
        )
        q = jnp.concatenate([q_ref[0], jnp.zeros((DH, tokens), jnp.bfloat16)], axis=0)
        kept = usable_ref[...] > 0.5
        scores = jnp.dot(kv, q, preferred_element_type=jnp.float32)
        scores = jnp.where(kept, scores, NEG)
        largest = jnp.max(scores, axis=0, keepdims=True)
        exponent = jnp.where(kept, jnp.exp(scores - largest), 0.0)
        weight = jnp.sum(exponent, axis=0, keepdims=True)
        sums = lax.dot_general(
            kv, exponent.astype(jnp.bfloat16), (((0,), (0,)), ((), ())),
            preferred_element_type=jnp.float32,
        )
        out_ref[0] = pack(sums[DH:], largest, weight)

    return pl.pallas_call(
        body,
        grid_spec=pltpu.PrefetchScalarGridSpec(
            num_scalar_prefetch=1,
            grid=(count,),
            in_specs=[
                pl.BlockSpec((1, DH, tokens), lambda i, c: (i, 0, 0)),
                pl.BlockSpec((requests, positions, lane), lambda i, c: (0, 0, c[0, i])),
                pl.BlockSpec((requests, positions, lane), lambda i, c: (0, 0, c[1, i])),
                pl.BlockSpec((2 * rows, tokens), lambda i, c: (0, 0)),
            ],
            out_specs=pl.BlockSpec((1, DH + 16, tokens), lambda i, c: (i, 0, 0)),
        ),
        out_shape=jax.ShapeDtypeStruct((count, DH + 16, tokens), jnp.bfloat16),
        name="partial_attention",
    )(columns, query, own, partner, usable)


def join_parts(*parts):
    def body(*refs):
        for n in range(parts[0].shape[0]):
            total = unpack(refs[0][n])
            for ref in refs[1:-1]:
                total = merge(total, unpack(ref[n]))
            refs[-1][n] = pack(*total)

    return pl.pallas_call(
        body, out_shape=jax.ShapeDtypeStruct(parts[0].shape, jnp.bfloat16), name="join_parts"
    )(*parts)


def close_parts(*parts):
    def body(*refs):
        total = unpack(refs[0][0])
        for ref in refs[1:-1]:
            total = merge(total, unpack(ref[0]))
        sums, _, weight = total
        refs[-1][...] = (sums / weight).astype(jnp.bfloat16)

    return pl.pallas_call(
        body,
        out_shape=jax.ShapeDtypeStruct((DH, parts[0].shape[2]), jnp.bfloat16),
        name="close_parts",
    )(*parts)


def token_order(tokens, chip, core):
    n = lax.broadcasted_iota(jnp.int32, (tokens, tokens), 1)
    m = lax.broadcasted_iota(jnp.int32, (tokens, tokens), 0)
    each = tokens // (2 * RING)
    slot = (n // (2 * each) - chip + RING) % RING
    near = slot % 8
    far = (slot // 8 + (near >= 5)) % 4
    half = ((n // each) % 2 != core).astype(jnp.int32)
    row = half * (tokens // 2) + (near * 4 + far) * each + n % each
    return (row == m).astype(jnp.bfloat16)


def per_device(
    hidden,
    norm_gain_attn,
    w_query,
    entering_kv,
    cached_kv,
    enc_lengths,
    w_out,
    norm_gain_ffn,
    w_gate,
    w_up,
    w_down,
):
    chip = lax.axis_index("mp_0").astype(jnp.int32)
    core = lax.axis_index("mp_1").astype(jnp.int32)
    rows, width = hidden.shape
    mine = RING * rows
    tokens = 2 * mine
    requests, positions, _ = entering_kv.shape

    partner_kv = other_core(every_second_head(entering_kv, (1 - core)[None]))
    order = token_order(tokens, chip, core)
    entered = tokens // 2
    place = jnp.arange(2 * requests * positions, dtype=jnp.int32)
    source = jnp.where(place // (requests * positions) == 0, core, 1 - core)
    at = (2 * chip + source) * positions + place % positions
    row_request = (place // positions) % requests
    in_length = at < jnp.take(enc_lengths[0], row_request)
    token_request = jnp.arange(entered, dtype=jnp.int32) // QLEN
    usable = (
        (row_request[:, None] == token_request[None, :]) & in_length[:, None]
    ).astype(jnp.float32)
    heads = (chip + jnp.array(SLOTS, jnp.int32)) % RING
    columns = jnp.stack([2 * heads + core, heads])

    def everyone(x):
        gathered = ring_gather(x).reshape(mine, width)
        return gathered, other_core(gathered)

    def query_of(x):
        return lax.dot_general(
            w_query, x, (((0,), (1,)), ((), ())), preferred_element_type=jnp.float32
        ).astype(jnp.bfloat16)

    normed_own, normed_other = everyone(normalize(hidden, norm_gain_attn))
    query = jnp.concatenate([query_of(normed_own), query_of(normed_other)], axis=1)
    query = jnp.dot(query, order, preferred_element_type=jnp.float32).astype(jnp.bfloat16)

    gathered_query = ring_gather(query[:, :entered])
    parts = partial_attention(gathered_query, entering_kv, partner_kv, usable, columns)
    context_entering = close_parts(*ring_reduce(parts, join_parts, join_parts, lambda x: x))
    context_cached = attend(query[:, entered:].T, cached_kv, enc_lengths[1]).T
    context = jnp.concatenate([context_entering, context_cached], axis=1)
    context = lax.dot_general(
        context, order, (((1,), (1,)), ((), ())), preferred_element_type=jnp.float32
    ).astype(jnp.bfloat16)

    def summed(product_of, own, other):
        arrived = other_core(product_of(other).astype(jnp.bfloat16))
        total = product_of(own) + arrived.astype(jnp.float32)
        return sum_over_ring(total.reshape(RING, rows, width))

    def out_product(x):
        return lax.dot_general(
            x, w_out, (((0,), (0,)), ((), ())), preferred_element_type=jnp.float32
        )

    attention = summed(out_product, context[:, :mine], context[:, mine:])
    residual = (hidden.astype(jnp.float32) + attention).astype(jnp.bfloat16)

    def feed(x):
        gate = jnp.dot(x, w_gate, preferred_element_type=jnp.float32)
        upward = jnp.dot(x, w_up, preferred_element_type=jnp.float32)
        activated = (jax.nn.gelu(gate, approximate=True) * upward).astype(jnp.bfloat16)
        return jnp.dot(activated, w_down, preferred_element_type=jnp.float32)

    feed_out = summed(feed, *everyone(normalize(residual, norm_gain_ffn)))
    return (residual.astype(jnp.float32) + feed_out).astype(jnp.bfloat16)


def solution(mesh):
    torus = Mesh(mesh.devices.reshape(mesh.shape["groups"], RING, 2), ("groups", "mp_0", "mp_1"))
    in_specs = (
        P(GROUPS_MP, None),
        P(),
        P(None, MP),
        P("groups", MP, None),
        P("groups", None, MP),
        P(None, "groups"),
        P(MP, None),
        P(),
        P(None, MP),
        P(None, MP),
        P(MP, None),
    )
    out_specs = P(GROUPS_MP, None)
    return jax.shard_map(
        per_device, mesh=torus, in_specs=in_specs, out_specs=out_specs, check_vma=False
    )
```

time: 1100 us -> 566 us (0.51)
  waiting for transfers between devices: 838 us -> 183 us
  starting transfers between devices: 35.2 us -> 231 us
  local copies, waits for them, and re-layouts: 172 us -> 39.3 us
  Pallas kernels: 0 us -> 49.5 us
  other arithmetic: 4.28 us -> 18.8 us
  between operations: 13.6 us -> 1.17 us
    all_gather x3 -> x0, waiting for transfers between devices: 441 us -> none  [the longest x2 310 us: all_blocks(): parts = lax.all_gather(parts, axes[k], axis=0, tiled=True)]
    reduce_scatter x4 -> x0, waiting for transfers between devices: 326 us -> none  [sum_in_order(): parts = lax.psum_scatter(parts, axes[k], scatter_dimension=0, tiled=True)]
    ppermute x0 -> x77, starting transfers between devices: none -> 231 us  [the longest x72 230 us: fetch(): return lax.ppermute(x, 'mp_0', [(i, (i - k) % RING) for i in range(RING)])]
    ppermute x0 -> x77, waiting for transfers between devices: none -> 183 us  [the longest x72 173 us: fetch(): return lax.ppermute(x, 'mp_0', [(i, (i - k) % RING) for i in range(RING)])]
    unnamed x22 -> x75, local copies, waits for them, and re-layouts: 107 us -> 27.9 us
    all_to_all x1 -> x0, waiting for transfers between devices: 70.5 us -> none  [per_device(): lax.all_to_all(entering_kv, MP, split_axis=2, concat_axis=1, tiled=True)]
    pallas_call x0 -> x13, Pallas kernels: none -> 49.5 us  [the longest x1 25.9 us: partial_attention(): pl.pallas_call(body, grid_spec=pltpu.PrefetchScalarGridSpec(num_scalar_pr...]
    all_to_all x1 -> x0, starting transfers between devices: 34.4 us -> none  [per_device(): lax.all_to_all(entering_kv, MP, split_axis=2, concat_axis=1, tiled=True)]
  transfers between devices with their start and end apart: 8 -> 77, of which waited for: 8 -> 49; matrix products, arithmetic and copies ran while one was open for 2% -> 9% of each run, Pallas kernels for 0% -> 4%
where the time goes in v1:
time: 566 us; the launch traced here: 555 us
  starting transfers between devices  231 us (41%)
  waiting for transfers between devices  183 us (32%)
  Pallas kernels  49.5 us (9%)
  local copies, waits for them, and re-layouts  39.3 us (7%)
  matrix products  32.1 us (6%)
  other arithmetic  18.8 us (3%)
    ppermute x72, starting transfers between devices, fetch(): return lax.ppermute(x, 'mp_0', [(i, (i - k) % RING) for i in range(RING)])  230 us
    ppermute x72, waiting for transfers between devices, fetch(): return lax.ppermute(x, 'mp_0', [(i, (i - k) % RING) for i in range(RING)])  173 us
    unnamed x75, local copies, waits for them, and re-layouts  27.9 us
    pallas_call x1, Pallas kernels, partial_attention(): pl.pallas_call(body, grid_spec=pltpu.PrefetchScalarGridSpec(num_scalar_pr...  25.9 us
    pallas_call x10, Pallas kernels, join_parts(): pl.pallas_call(body, out_shape=jax.ShapeDtypeStruct(parts[0].shape, jnp.b...  16.3 us
    dot_general x2, matrix products, feed(): return jnp.dot(activated, w_down, preferred_element_type=jnp.float32)  13.3 us
  transfers between devices with their start and end apart: 77, of which 49 were waited for; matrix products, arithmetic and copies ran while one was open for 9% of the time, Pallas kernels for 4%

profile of v1, /device:TPU:38, one launch (start us, length us, event | category | flops | bytes accessed | tf_op | source)
XLA Modules:
  0.0 555.1 jit_solution(1246591557670667124)
XLA Ops:
  2.7 15.4 %collective-permute-start.2 = (bf16[8,4096]{1,0:T(8,128)(2,1)S(1)}, bf16[8,4096]{1,0:T(8,128)(2,1)S(1)}, u32[]{:S(2)}, u32[]{:S(2)}) collective-permute-start(bf16[8,4096]{1,0:T(8,128)(2,1)S(1)} %get-tuple-element.16), channel_id=1, source_target_pairs={{0,16},{2,18},{4,20},{6,22},{8,24},{10,26},{12,28},{14,30},{16,32}... | collective-permute-start | bytes 196616 | tf_op jit(solution)/shard_map/ppermute | solution.py:23
  18.1 10.5 %collective-permute-start = (bf16[8,4096]{1,0:T(8,128)(2,1)S(1)}, bf16[8,4096]{1,0:T(8,128)(2,1)S(1)}, u32[]{:S(2)}, u32[]{:S(2)}) collective-permute-start(bf16[8,4096]{1,0:T(8,128)(2,1)S(1)} %get-tuple-element.16), channel_id=1, source_target_pairs={{0,48},{2,50},{4,52},{6,54},{8,56},{10,58},{12,60},{14,62},{16,0},... | collective-permute-start | bytes 196616 | tf_op jit(solution)/shard_map/ppermute | solution.py:23
  31.3 9.7 %collective-permute-start.3 = (bf16[8,2048]{1,0:T(8,128)(2,1)S(1)}, bf16[8,2048]{1,0:T(8,128)(2,1)S(1)}, u32[]{:S(2)}, u32[]{:S(2)}) collective-permute-start(bf16[8,2048]{1,0:T(8,128)(2,1)S(1)} %slice.496), channel_id=1, source_target_pairs={{0,16},{2,18},{4,20},{6,22},{8,24},{10,26},{12,28},{14,30},{16,32}... | collective-permute-start | bytes 98312 | tf_op jit(solution)/shard_map/ppermute | solution.py:23
  41.0 3.6 collective-permute-done
  44.7 4.1 collective-permute-start.1
  50.8 8.3 %collective-permute-done.1 = bf16[8,2048]{1,0:T(8,128)(2,1)S(1)} collective-permute-done((bf16[8,2048]{1,0:T(8,128)(2,1)S(1)}, bf16[8,2048]{1,0:T(8,128)(2,1)S(1)}, u32[]{:S(2)}, u32[]{:S(2)}) %collective-permute-start.1) | collective-permute-done | bytes 32800 | tf_op jit(solution)/shard_map/ppermute | solution.py:23
  63.7 4.8 collective-permute-done.8
  72.4 4.5 collective-permute-done.9
  80.9 3.6 collective-permute-done.10
  84.7 3.3 collective-permute-start.7
  94.0 5.8 %every_second_head.1 = bf16[8,32,4096]{2,1,0:T(8,128)(2,1)} custom-call(s32[1]{0:T(128)} %bitcast.13.parity_ref, bf16[8,32,8192]{2,1,0:T(8,128)(2,1)} %own_ref.1, bf16[8,32,8192]{2,1,0:T(8,128)(2,1)} %own_ref.1, bf16[8,32,8192]{2,1,0:T(8,128)(2,1)} %own_ref.1, bf16[8,32,8192]{2,1,0:T(8,128)(2,1)} %own_ref.1), custom_call_target="tpu_custom_call" | custom-call | tf_op jit(solution)/shard_map/every_second_head/pallas_call | solution.py:123
  101.3 4.4 compare_select_fusion.3
  112.5 6.3 %collective-permute-start.13 = (bf16[64,256]{1,0:T(8,128)(2,1)S(1)}, bf16[64,256]{1,0:T(8,128)(2,1)S(1)}, u32[]{:S(2)}, u32[]{:S(2)}) collective-permute-start(bf16[64,256]{1,0:T(8,128)(2,1)S(1)} %get-tuple-element.73), channel_id=1, source_target_pairs={{0,48},{2,50},{4,52},{6,54},{8,56},{10,58},{12,60},{14,62},{16,0},... | collective-permute-start | bytes 98312 | tf_op jit(solution)/shard_map/ppermute | solution.py:23
  118.7 4.6 collective-permute-start.15
  125.6 7.5 %collective-permute-start.14 = (bf16[64,128]{1,0:T(8,128)(2,1)S(1)}, bf16[64,128]{1,0:T(8,128)(2,1)S(1)}, u32[]{:S(2)}, u32[]{:S(2)}) collective-permute-start(bf16[64,128]{1,0:T(8,128)(2,1)S(1)} %slice.501), channel_id=1, source_target_pairs={{0,48},{2,50},{4,52},{6,54},{8,56},{10,58},{12,60},{14,62},{16,0},... | collective-permute-start | bytes 49160 | tf_op jit(solution)/shard_map/ppermute | solution.py:23
  134.1 4.1 collective-permute-start.16
  138.8 7.8 %collective-permute-done.16 = bf16[64,128]{1,0:T(8,128)(2,1)S(1)} collective-permute-done((bf16[64,128]{1,0:T(8,128)(2,1)S(1)}, bf16[64,128]{1,0:T(8,128)(2,1)S(1)}, u32[]{:S(2)}, u32[]{:S(2)}) %collective-permute-start.16) | collective-permute-done | bytes 16416 | tf_op jit(solution)/shard_map/ppermute | solution.py:23
  146.7 3.6 collective-permute-start.17
  153.2 3.4 collective-permute-start.18
  166.4 3.7 collective-permute-start.20
  176.6 25.9 %partial_attention.1 = bf16[32,80,256]{2,1,0:T(8,128)(2,1)} custom-call(s32[2,32]{1,0:T(2,128)} %pad_add_fusion.columns_ref, bf16[32,64,256]{2,1,0:T(8,128)(2,1)} %constant_dynamic-update-slice_fusion.12.q_ref, bf16[8,32,8192]{2,1,0:T(8,128)(2,1)} %own_ref.1, bf16[8,32,4096]{2,1,0:T(8,128)(2,1)} %copy-done.5, f32[512,256]{1,0:T(8,128)} %and_convert_fusion.usable_ref), custom_call_target="tpu_custom_call" | custom-call | tf_op jit(solution)/shard_map/partial_attention/pallas_call | solution.py:193
  205.9 3.6 collective-permute-start.30
  218.2 3.3 collective-permute-start.31
  228.1 3.7 collective-permute-start.32
  238.5 3.6 collective-permute-start.33
  242.1 6.6 %copy.16 = bf16[8,2048,128]{1,2,0:T(8,128)(2,1)} copy(bf16[8,2048,128]{2,1,0:T(8,128)(2,1)} %param.16) | data formatting | bytes 8388608 | tf_op args[4]
  252.9 3.5 collective-permute-start.34
  256.5 3.8 fusion.165
  260.3 7.2 %collective-permute-start.36 = (bf16[1,80,128]{2,1,0:T(8,128)(2,1)S(1)}, bf16[1,80,128]{2,1,0:T(8,128)(2,1)S(1)}, u32[]{:S(2)}, u32[]{:S(2)}) collective-permute-start(bf16[1,80,128]{2,1,0:T(8,128)(2,1)S(1)} %get-tuple-element.62), channel_id=1, source_target_pairs={{0,48},{2,50},{4,52},{6,54},{8,56},{10,58},{12,60},{14,62},{16,0},... | collective-permute-start | bytes 61448 | tf_op jit(solution)/shard_map/ppermute | solution.py:23
  270.2 3.5 collective-permute-start.35
  276.5 7.6 %collective-permute-start.37 = (bf16[1,80,256]{2,1,0:T(8,128)(2,1)S(1)}, bf16[1,80,256]{2,1,0:T(8,128)(2,1)S(1)}, u32[]{:S(2)}, u32[]{:S(2)}) collective-permute-start(bf16[1,80,256]{2,1,0:T(8,128)(2,1)S(1)} %pad_maximum_fusion.17), channel_id=1, source_target_pairs={{0,48},{2,50},{4,52},{6,54},{8,56},{10,58},{12,60},{14,62},{16,0},... | collective-permute-start | bytes 122888 | tf_op jit(solution)/shard_map/ppermute | solution.py:23
  293.8 4.1 collective-permute-done.38
  302.0 3.5 collective-permute-done.39
  305.8 3.3 collective-permute-start.44
  309.2 5.3 collective-permute-done.40
  314.6 7.8 %collective-permute-done.41 = bf16[4,8,4096]{2,1,0:T(8,128)(2,1)S(1)} collective-permute-done((bf16[4,8,4096]{2,1,0:T(8,128)(2,1)S(1)}, bf16[4,8,4096]{2,1,0:T(8,128)(2,1)S(1)}, u32[]{:S(2)}, u32[]{:S(2)}) %collective-permute-start.41) | collective-permute-done | bytes 262176 | tf_op jit(solution)/shard_map/ppermute | solution.py:23
  324.7 5.1 collective-permute-done.45
  330.5 5.9 %collective-permute-done.46 = bf16[4,8,4096]{2,1,0:T(8,128)(2,1)S(1)} collective-permute-done((bf16[4,8,4096]{2,1,0:T(8,128)(2,1)S(1)}, bf16[4,8,4096]{2,1,0:T(8,128)(2,1)S(1)}, u32[]{:S(2)}, u32[]{:S(2)}) %collective-permute-start.46) | collective-permute-done | bytes 262176 | tf_op jit(solution)/shard_map/ppermute | solution.py:23
  336.6 8.1 %collective-permute-start.47 = (bf16[1,8,2048]{2,1,0:T(8,128)(2,1)S(1)}, bf16[1,8,2048]{2,1,0:T(8,128)(2,1)S(1)}, u32[]{:S(2)}, u32[]{:S(2)}) collective-permute-start(bf16[1,8,2048]{2,1,0:T(8,128)(2,1)S(1)} %get-tuple-element.55), channel_id=1, source_target_pairs={{0,16},{2,18},{4,20},{6,22},{8,24},{10,26},{12,28},{14,30},{16,32}... | collective-permute-start | bytes 98312 | tf_op jit(solution)/shard_map/ppermute | solution.py:23
  350.1 7.5 %collective-permute-done.49 = bf16[1,8,2048]{2,1,0:T(8,128)(2,1)S(1)} collective-permute-done((bf16[1,8,2048]{2,1,0:T(8,128)(2,1)S(1)}, bf16[1,8,2048]{2,1,0:T(8,128)(2,1)S(1)}, u32[]{:S(2)}, u32[]{:S(2)}) %collective-permute-start.49) | collective-permute-done | bytes 32800 | tf_op jit(solution)/shard_map/ppermute | solution.py:23
  360.3 8.4 %collective-permute-start.48 = (bf16[1,8,4096]{2,1,0:T(8,128)(2,1)S(1)}, bf16[1,8,4096]{2,1,0:T(8,128)(2,1)S(1)}, u32[]{:S(2)}, u32[]{:S(2)}) collective-permute-start(bf16[1,8,4096]{2,1,0:T(8,128)(2,1)S(1)} %pad_maximum_fusion.12), channel_id=1, source_target_pairs={{0,16},{2,18},{4,20},{6,22},{8,24},{10,26},{12,28},{14,30},{16,32}... | collective-permute-start | bytes 196616 | tf_op jit(solution)/shard_map/ppermute | solution.py:23
  368.7 4.9 collective-permute-done.50
  375.3 8.5 %collective-permute-start.53 = (bf16[8,4096]{1,0:T(8,128)(2,1)S(1)}, bf16[8,4096]{1,0:T(8,128)(2,1)S(1)}, u32[]{:S(2)}, u32[]{:S(2)}) collective-permute-start(bf16[8,4096]{1,0:T(8,128)(2,1)S(1)} %get-tuple-element.8), channel_id=1, source_target_pairs={{0,16},{2,18},{4,20},{6,22},{8,24},{10,26},{12,28},{14,30},{16,32}... | collective-permute-start | bytes 196616 | tf_op jit(solution)/shard_map/ppermute | solution.py:23
  388.7 8.1 %collective-permute-start.54 = (bf16[8,2048]{1,0:T(8,128)(2,1)S(1)}, bf16[8,2048]{1,0:T(8,128)(2,1)S(1)}, u32[]{:S(2)}, u32[]{:S(2)}) collective-permute-start(bf16[8,2048]{1,0:T(8,128)(2,1)S(1)} %slice.554), channel_id=1, source_target_pairs={{0,16},{2,18},{4,20},{6,22},{8,24},{10,26},{12,28},{14,30},{16,32}... | collective-permute-start | bytes 98312 | tf_op jit(solution)/shard_map/ppermute | solution.py:23
  396.8 3.6 collective-permute-start.52
  401.3 9.2 %collective-permute-done.52 = bf16[8,2048]{1,0:T(8,128)(2,1)S(1)} collective-permute-done((bf16[8,2048]{1,0:T(8,128)(2,1)S(1)}, bf16[8,2048]{1,0:T(8,128)(2,1)S(1)}, u32[]{:S(2)}, u32[]{:S(2)}) %collective-permute-start.52) | collective-permute-done | bytes 32800 | tf_op jit(solution)/shard_map/ppermute | solution.py:23
  410.5 4.5 collective-permute-start.59
  418.0 5.8 %collective-permute-done.59 = bf16[4,8,4096]{2,1,0:T(8,128)(2,1)S(1)} collective-permute-done((bf16[4,8,4096]{2,1,0:T(8,128)(2,1)S(1)}, bf16[4,8,4096]{2,1,0:T(8,128)(2,1)S(1)}, u32[]{:S(2)}, u32[]{:S(2)}) %collective-permute-start.59) | collective-permute-done | bytes 262176 | tf_op jit(solution)/shard_map/ppermute | solution.py:23
  427.1 5.7 %collective-permute-done.60 = bf16[4,8,4096]{2,1,0:T(8,128)(2,1)S(1)} collective-permute-done((bf16[4,8,4096]{2,1,0:T(8,128)(2,1)S(1)}, bf16[4,8,4096]{2,1,0:T(8,128)(2,1)S(1)}, u32[]{:S(2)}, u32[]{:S(2)}) %collective-permute-start.60) | collective-permute-done | bytes 262176 | tf_op jit(solution)/shard_map/ppermute | solution.py:23
  436.1 4.3 collective-permute-done.61
  447.2 4.1 collective-permute-done.63
  454.2 5.8 %convolution_convert_fusion = bf16[256,4096]{1,0:T(8,128)(2,1)} fusion(bf16[160,4096]{1,0:T(8,128)(2,1)S(1)} %copy-done, f32[256,160]{0,1:T(8,128)} %fusion.172, bf16[256,4096]{1,0:T(8,128)(2,1)} %copy-done.2, bf16[4096,160]{0,1:T(8,128)(2,1)} %param.21), kind=kOutput, calls=%fused_computation.1 | convolution fusion | flops 672546816 | bytes 6979584 | tf_op jit(solution)/shard_map/dot_general | solution.py:325
  464.6 7.4 %fusion.167 = (bf16[256,4096]{1,0:T(8,128)(2,1)}, f32[256,4096]{1,0:T(8,128)}) fusion(bf16[256,4096]{1,0:T(8,128)(2,1)} %collective-permute-done.64, bf16[160,4096]{1,0:T(8,128)(2,1)S(1)} %copy-done, f32[256,160]{0,1:T(8,128)} %fusion.128, bf16[4096,160]{0,1:T(8,128)(2,1)} %param.20, bf16[32,8,4096]{2,1,0:T(8,128)(2,1)S(1)} %constant_dynamic-update-slice_fusion.24), kind=kOutput, calls=%fused_computation.324 | convolution fusion | flops 674643968 | bytes 13271040 | tf_op jit(solution)/shard_map/dot_general | solution.py:325
  473.4 3.5 collective-permute-start.69
  476.9 3.7 collective-permute-done.65
  482.8 3.3 collective-permute-start.70
  486.1 4.6 collective-permute-done.66
  492.0 8.1 %collective-permute-done.67 = bf16[4,8,4096]{2,1,0:T(8,128)(2,1)S(1)} collective-permute-done((bf16[4,8,4096]{2,1,0:T(8,128)(2,1)S(1)}, bf16[4,8,4096]{2,1,0:T(8,128)(2,1)S(1)}, u32[]{:S(2)}, u32[]{:S(2)}) %collective-permute-start.67) | collective-permute-done | bytes 262176 | tf_op jit(solution)/shard_map/ppermute | solution.py:23
  502.3 4.6 collective-permute-done.71
  508.3 5.4 collective-permute-done.72
  513.8 9.6 %collective-permute-start.73 = (bf16[1,8,2048]{2,1,0:T(8,128)(2,1)S(1)}, bf16[1,8,2048]{2,1,0:T(8,128)(2,1)S(1)}, u32[]{:S(2)}, u32[]{:S(2)}) collective-permute-start(bf16[1,8,2048]{2,1,0:T(8,128)(2,1)S(1)} %get-tuple-element.49), channel_id=1, source_target_pairs={{0,16},{2,18},{4,20},{6,22},{8,24},{10,26},{12,28},{14,30},{16,32}... | collective-permute-start | bytes 98312 | tf_op jit(solution)/shard_map/ppermute | solution.py:23
  527.5 8.6 %collective-permute-done.75 = bf16[1,8,2048]{2,1,0:T(8,128)(2,1)S(1)} collective-permute-done((bf16[1,8,2048]{2,1,0:T(8,128)(2,1)S(1)}, bf16[1,8,2048]{2,1,0:T(8,128)(2,1)S(1)}, u32[]{:S(2)}, u32[]{:S(2)}) %collective-permute-start.75) | collective-permute-done | bytes 32800 | tf_op jit(solution)/shard_map/ppermute | solution.py:23
  537.5 9.5 %collective-permute-start.74 = (bf16[1,8,4096]{2,1,0:T(8,128)(2,1)S(1)}, bf16[1,8,4096]{2,1,0:T(8,128)(2,1)S(1)}, u32[]{:S(2)}, u32[]{:S(2)}) collective-permute-start(bf16[1,8,4096]{2,1,0:T(8,128)(2,1)S(1)} %pad_maximum_fusion.14), channel_id=1, source_target_pairs={{0,16},{2,18},{4,20},{6,22},{8,24},{10,26},{12,28},{14,30},{16,32}... | collective-permute-start | bytes 196616 | tf_op jit(solution)/shard_map/ppermute | solution.py:23
  547.0 4.3 collective-permute-done.76
  (279 shorter events, 166.2 us)
Async XLA Ops:
  2.7 28.7 %collective-permute-start.2 = (bf16[8,4096]{1,0:T(8,128)(2,1)S(1)}, bf16[8,4096]{1,0:T(8,128)(2,1)S(1)}, u32[]{:S(2)}, u32[]{:S(2)}) collective-permute-start(bf16[8,4096]{1,0:T(8,128)(2,1)S(1)} %get-tuple-element.16), channel_id=1, source_target_pairs={{0,16},{2,18},{4,20},{6,22},{8,24},{10,26},{12,28},{14,30},{16,32}... | collective-permute-start | bytes 196616 | tf_op jit(solution)/shard_map/ppermute | solution.py:23
  18.1 26.6 %collective-permute-start = (bf16[8,4096]{1,0:T(8,128)(2,1)S(1)}, bf16[8,4096]{1,0:T(8,128)(2,1)S(1)}, u32[]{:S(2)}, u32[]{:S(2)}) collective-permute-start(bf16[8,4096]{1,0:T(8,128)(2,1)S(1)} %get-tuple-element.16), channel_id=1, source_target_pairs={{0,48},{2,50},{4,52},{6,54},{8,56},{10,58},{12,60},{14,62},{16,0},... | collective-permute-start | bytes 196616 | tf_op jit(solution)/shard_map/ppermute | solution.py:23
  31.3 19.4 %collective-permute-start.3 = (bf16[8,2048]{1,0:T(8,128)(2,1)S(1)}, bf16[8,2048]{1,0:T(8,128)(2,1)S(1)}, u32[]{:S(2)}, u32[]{:S(2)}) collective-permute-start(bf16[8,2048]{1,0:T(8,128)(2,1)S(1)} %slice.496), channel_id=1, source_target_pairs={{0,16},{2,18},{4,20},{6,22},{8,24},{10,26},{12,28},{14,30},{16,32}... | collective-permute-start | bytes 98312 | tf_op jit(solution)/shard_map/ppermute | solution.py:23
  44.7 14.4 %collective-permute-start.1 = (bf16[8,2048]{1,0:T(8,128)(2,1)S(1)}, bf16[8,2048]{1,0:T(8,128)(2,1)S(1)}, u32[]{:S(2)}, u32[]{:S(2)}) collective-permute-start(bf16[8,2048]{1,0:T(8,128)(2,1)S(1)} %slice.495), channel_id=1, source_target_pairs={{0,48},{2,50},{4,52},{6,54},{8,56},{10,58},{12,60},{14,62},{16,0},... | collective-permute-start | bytes 98312 | tf_op jit(solution)/shard_map/ppermute | solution.py:23
  59.1 9.4 %collective-permute-start.8 = (bf16[4,8,4096]{2,1,0:T(8,128)(2,1)S(1)}, bf16[4,8,4096]{2,1,0:T(8,128)(2,1)S(1)}, u32[]{:S(2)}, u32[]{:S(2)}) collective-permute-start(bf16[4,8,4096]{2,1,0:T(8,128)(2,1)S(1)} %pad_maximum_fusion), channel_id=1, source_target_pairs={{0,2},{2,4},{4,6},{6,8},{8,10},{10,12},{12,14},{14,16},{16,18},{18... | collective-permute-start | bytes 786440 | tf_op jit(solution)/shard_map/ppermute | solution.py:23
  59.2 9.3 %collective-permute-start.4 = (bf16[4,8,4096]{2,1,0:T(8,128)(2,1)S(1)}, bf16[4,8,4096]{2,1,0:T(8,128)(2,1)S(1)}, u32[]{:S(2)}, u32[]{:S(2)}) collective-permute-start(bf16[4,8,4096]{2,1,0:T(8,128)(2,1)S(1)} %pad_maximum_fusion), channel_id=1, source_target_pairs={{0,62},{2,0},{4,2},{6,4},{8,6},{10,8},{12,10},{14,12},{16,14},{18,... | collective-permute-start | bytes 786440 | tf_op jit(solution)/shard_map/ppermute | solution.py:23
  68.5 8.4 %collective-permute-start.9 = (bf16[4,8,4096]{2,1,0:T(8,128)(2,1)S(1)}, bf16[4,8,4096]{2,1,0:T(8,128)(2,1)S(1)}, u32[]{:S(2)}, u32[]{:S(2)}) collective-permute-start(bf16[4,8,4096]{2,1,0:T(8,128)(2,1)S(1)} %collective-permute-done.8), channel_id=1, source_target_pairs={{0,2},{2,4},{4,6},{6,8},{8,10},{10,12},{12,14},{14,16},{16,18},{18... | collective-permute-start | bytes 786440 | tf_op jit(solution)/shard_map/ppermute | solution.py:23
  68.5 8.4 %collective-permute-start.5 = (bf16[4,8,4096]{2,1,0:T(8,128)(2,1)S(1)}, bf16[4,8,4096]{2,1,0:T(8,128)(2,1)S(1)}, u32[]{:S(2)}, u32[]{:S(2)}) collective-permute-start(bf16[4,8,4096]{2,1,0:T(8,128)(2,1)S(1)} %collective-permute-done.4), channel_id=1, source_target_pairs={{0,62},{2,0},{4,2},{6,4},{8,6},{10,8},{12,10},{14,12},{16,14},{18,... | collective-permute-start | bytes 786440 | tf_op jit(solution)/shard_map/ppermute | solution.py:23
  76.9 7.6 %collective-permute-start.10 = (bf16[4,8,4096]{2,1,0:T(8,128)(2,1)S(1)}, bf16[4,8,4096]{2,1,0:T(8,128)(2,1)S(1)}, u32[]{:S(2)}, u32[]{:S(2)}) collective-permute-start(bf16[4,8,4096]{2,1,0:T(8,128)(2,1)S(1)} %collective-permute-done.9), channel_id=1, source_target_pairs={{0,2},{2,4},{4,6},{6,8},{8,10},{10,12},{12,14},{14,16},{16,18},{18... | collective-permute-start | bytes 786440 | tf_op jit(solution)/shard_map/ppermute | solution.py:23
  76.9 7.8 %collective-permute-start.6 = (bf16[4,8,4096]{2,1,0:T(8,128)(2,1)S(1)}, bf16[4,8,4096]{2,1,0:T(8,128)(2,1)S(1)}, u32[]{:S(2)}, u32[]{:S(2)}) collective-permute-start(bf16[4,8,4096]{2,1,0:T(8,128)(2,1)S(1)} %collective-permute-done.5), channel_id=1, source_target_pairs={{0,62},{2,0},{4,2},{6,4},{8,6},{10,8},{12,10},{14,12},{16,14},{18,... | collective-permute-start | bytes 786440 | tf_op jit(solution)/shard_map/ppermute | solution.py:23
  84.5 6.7 %collective-permute-start.11 = (bf16[2,8,4096]{2,1,0:T(8,128)(2,1)S(1)}, bf16[2,8,4096]{2,1,0:T(8,128)(2,1)S(1)}, u32[]{:S(2)}, u32[]{:S(2)}) collective-permute-start(bf16[2,8,4096]{2,1,0:T(8,128)(2,1)S(1)} %pad_maximum_fusion.8), channel_id=1, source_target_pairs={{0,2},{2,4},{4,6},{6,8},{8,10},{10,12},{12,14},{14,16},{16,18},{18... | collective-permute-start | bytes 393224 | tf_op jit(solution)/shard_map/ppermute | solution.py:23
  94.0 15.8 %collective-permute-start.12 = (bf16[256,4096]{1,0:T(8,128)(2,1)}, bf16[256,4096]{1,0:T(8,128)(2,1)}, u32[]{:S(2)}, u32[]{:S(2)}) collective-permute-start(bf16[256,4096]{1,0:T(8,128)(2,1)} %bitcast.6), channel_id=1, source_target_pairs={{0,1},{1,0},{2,3},{3,2},{4,5},{5,4},{6,7},{7,6},{8,9},{9,8},{10,11... | collective-permute-start | bytes 6291464 | tf_op jit(solution)/shard_map/ppermute | solution.py:27
  99.9 75.4 %collective-permute-start.25 = (bf16[8,32,4096]{2,1,0:T(8,128)(2,1)}, bf16[8,32,4096]{2,1,0:T(8,128)(2,1)S(1)}, u32[]{:S(2)}, u32[]{:S(2)}) collective-permute-start(bf16[8,32,4096]{2,1,0:T(8,128)(2,1)} %every_second_head.1), channel_id=1, source_target_pairs={{0,1},{1,0},{2,3},{3,2},{4,5},{5,4},{6,7},{7,6},{8,9},{9,8},{10,11... | collective-permute-start | bytes 6291464 | tf_op jit(solution)/shard_map/ppermute | solution.py:27
  112.5 13.2 %collective-permute-start.13 = (bf16[64,256]{1,0:T(8,128)(2,1)S(1)}, bf16[64,256]{1,0:T(8,128)(2,1)S(1)}, u32[]{:S(2)}, u32[]{:S(2)}) collective-permute-start(bf16[64,256]{1,0:T(8,128)(2,1)S(1)} %get-tuple-element.73), channel_id=1, source_target_pairs={{0,48},{2,50},{4,52},{6,54},{8,56},{10,58},{12,60},{14,62},{16,0},... | collective-permute-start | bytes 98312 | tf_op jit(solution)/shard_map/ppermute | solution.py:23
  118.7 15.4 %collective-permute-start.15 = (bf16[64,256]{1,0:T(8,128)(2,1)S(1)}, bf16[64,256]{1,0:T(8,128)(2,1)S(1)}, u32[]{:S(2)}, u32[]{:S(2)}) collective-permute-start(bf16[64,256]{1,0:T(8,128)(2,1)S(1)} %get-tuple-element.73), channel_id=1, source_target_pairs={{0,16},{2,18},{4,20},{6,22},{8,24},{10,26},{12,28},{14,30},{16,32}... | collective-permute-start | bytes 98312 | tf_op jit(solution)/shard_map/ppermute | solution.py:23
  125.6 13.2 %collective-permute-start.14 = (bf16[64,128]{1,0:T(8,128)(2,1)S(1)}, bf16[64,128]{1,0:T(8,128)(2,1)S(1)}, u32[]{:S(2)}, u32[]{:S(2)}) collective-permute-start(bf16[64,128]{1,0:T(8,128)(2,1)S(1)} %slice.501), channel_id=1, source_target_pairs={{0,48},{2,50},{4,52},{6,54},{8,56},{10,58},{12,60},{14,62},{16,0},... | collective-permute-start | bytes 49160 | tf_op jit(solution)/shard_map/ppermute | solution.py:23
  134.1 12.5 %collective-permute-start.16 = (bf16[64,128]{1,0:T(8,128)(2,1)S(1)}, bf16[64,128]{1,0:T(8,128)(2,1)S(1)}, u32[]{:S(2)}, u32[]{:S(2)}) collective-permute-start(bf16[64,128]{1,0:T(8,128)(2,1)S(1)} %slice.502), channel_id=1, source_target_pairs={{0,16},{2,18},{4,20},{6,22},{8,24},{10,26},{12,28},{14,30},{16,32}... | collective-permute-start | bytes 49160 | tf_op jit(solution)/shard_map/ppermute | solution.py:23
  146.6 6.5 %collective-permute-start.21 = (bf16[4,64,256]{2,1,0:T(8,128)(2,1)S(1)}, bf16[4,64,256]{2,1,0:T(8,128)(2,1)S(1)}, u32[]{:S(2)}, u32[]{:S(2)}) collective-permute-start(bf16[4,64,256]{2,1,0:T(8,128)(2,1)S(1)} %pad_maximum_fusion.9), channel_id=1, source_target_pairs={{0,2},{2,4},{4,6},{6,8},{8,10},{10,12},{12,14},{14,16},{16,18},{18... | collective-permute-start | bytes 393224 | tf_op jit(solution)/shard_map/ppermute | solution.py:23
  153.2 6.9 %collective-permute-start.18 = (bf16[4,64,256]{2,1,0:T(8,128)(2,1)S(1)}, bf16[4,64,256]{2,1,0:T(8,128)(2,1)S(1)}, u32[]{:S(2)}, u32[]{:S(2)}) collective-permute-start(bf16[4,64,256]{2,1,0:T(8,128)(2,1)S(1)} %collective-permute-done.17), channel_id=1, source_target_pairs={{0,62},{2,0},{4,2},{6,4},{8,6},{10,8},{12,10},{14,12},{16,14},{18,... | collective-permute-start | bytes 393224 | tf_op jit(solution)/shard_map/ppermute | solution.py:23
  159.3 6.9 %collective-permute-start.23 = (bf16[4,64,256]{2,1,0:T(8,128)(2,1)S(1)}, bf16[4,64,256]{2,1,0:T(8,128)(2,1)S(1)}, u32[]{:S(2)}, u32[]{:S(2)}) collective-permute-start(bf16[4,64,256]{2,1,0:T(8,128)(2,1)S(1)} %collective-permute-done.22), channel_id=1, source_target_pairs={{0,2},{2,4},{4,6},{6,8},{8,10},{10,12},{12,14},{14,16},{16,18},{18... | collective-permute-start | bytes 393224 | tf_op jit(solution)/shard_map/ppermute | solution.py:23
  205.9 7.9 %collective-permute-start.30 = (bf16[2,80,256]{2,1,0:T(8,128)(2,1)S(1)}, bf16[2,80,256]{2,1,0:T(8,128)(2,1)S(1)}, u32[]{:S(2)}, u32[]{:S(2)}) collective-permute-start(bf16[2,80,256]{2,1,0:T(8,128)(2,1)S(1)} %get-tuple-element.36), channel_id=1, source_target_pairs={{0,62},{2,0},{4,2},{6,4},{8,6},{10,8},{12,10},{14,12},{16,14},{18,... | collective-permute-start | bytes 245768 | tf_op jit(solution)/shard_map/ppermute | solution.py:23
  213.7 8.8 %collective-permute-start.27 = (bf16[4,80,256]{2,1,0:T(8,128)(2,1)S(1)}, bf16[4,80,256]{2,1,0:T(8,128)(2,1)S(1)}, u32[]{:S(2)}, u32[]{:S(2)}) collective-permute-start(bf16[4,80,256]{2,1,0:T(8,128)(2,1)S(1)} %pad_maximum_fusion.6), channel_id=1, source_target_pairs={{0,2},{2,4},{4,6},{6,8},{8,10},{10,12},{12,14},{14,16},{16,18},{18... | collective-permute-start | bytes 491528 | tf_op jit(solution)/shard_map/ppermute | solution.py:23
  218.2 7.4 %collective-permute-start.31 = (bf16[4,80,256]{2,1,0:T(8,128)(2,1)S(1)}, bf16[4,80,256]{2,1,0:T(8,128)(2,1)S(1)}, u32[]{:S(2)}, u32[]{:S(2)}) collective-permute-start(bf16[4,80,256]{2,1,0:T(8,128)(2,1)S(1)} %pad_maximum_fusion.7), channel_id=1, source_target_pairs={{0,62},{2,0},{4,2},{6,4},{8,6},{10,8},{12,10},{14,12},{16,14},{18,... | collective-permute-start | bytes 491528 | tf_op jit(solution)/shard_map/ppermute | solution.py:23
  224.9 8.0 %collective-permute-start.28 = (bf16[4,80,256]{2,1,0:T(8,128)(2,1)}, bf16[4,80,256]{2,1,0:T(8,128)(2,1)S(1)}, u32[]{:S(2)}, u32[]{:S(2)}) collective-permute-start(bf16[4,80,256]{2,1,0:T(8,128)(2,1)} %join_parts.11), channel_id=1, source_target_pairs={{0,2},{2,4},{4,6},{6,8},{8,10},{10,12},{12,14},{14,16},{16,18},{18... | collective-permute-start | bytes 491528 | tf_op jit(solution)/shard_map/ppermute | solution.py:23
  228.1 7.9 %collective-permute-start.32 = (bf16[4,80,256]{2,1,0:T(8,128)(2,1)}, bf16[4,80,256]{2,1,0:T(8,128)(2,1)S(1)}, u32[]{:S(2)}, u32[]{:S(2)}) collective-permute-start(bf16[4,80,256]{2,1,0:T(8,128)(2,1)} %join_parts.15), channel_id=1, source_target_pairs={{0,62},{2,0},{4,2},{6,4},{8,6},{10,8},{12,10},{14,12},{16,14},{18,... | collective-permute-start | bytes 491528 | tf_op jit(solution)/shard_map/ppermute | solution.py:23
  235.3 13.5 %collective-permute-start.29 = (bf16[4,80,256]{2,1,0:T(8,128)(2,1)}, bf16[4,80,256]{2,1,0:T(8,128)(2,1)S(1)}, u32[]{:S(2)}, u32[]{:S(2)}) collective-permute-start(bf16[4,80,256]{2,1,0:T(8,128)(2,1)} %join_parts.12), channel_id=1, source_target_pairs={{0,2},{2,4},{4,6},{6,8},{8,10},{10,12},{12,14},{14,16},{16,18},{18... | collective-permute-start | bytes 491528 | tf_op jit(solution)/shard_map/ppermute | solution.py:23
  238.5 10.4 %collective-permute-start.33 = (bf16[4,80,256]{2,1,0:T(8,128)(2,1)}, bf16[4,80,256]{2,1,0:T(8,128)(2,1)S(1)}, u32[]{:S(2)}, u32[]{:S(2)}) collective-permute-start(bf16[4,80,256]{2,1,0:T(8,128)(2,1)} %join_parts.16), channel_id=1, source_target_pairs={{0,62},{2,0},{4,2},{6,4},{8,6},{10,8},{12,10},{14,12},{16,14},{18,... | collective-permute-start | bytes 491528 | tf_op jit(solution)/shard_map/ppermute | solution.py:23
  252.9 14.6 %collective-permute-start.34 = (bf16[1,80,128]{2,1,0:T(8,128)(2,1)S(1)}, bf16[1,80,128]{2,1,0:T(8,128)(2,1)S(1)}, u32[]{:S(2)}, u32[]{:S(2)}) collective-permute-start(bf16[1,80,128]{2,1,0:T(8,128)(2,1)S(1)} %get-tuple-element.65), channel_id=1, source_target_pairs={{0,16},{2,18},{4,20},{6,22},{8,24},{10,26},{12,28},{14,30},{16,32}... | collective-permute-start | bytes 61448 | tf_op jit(solution)/shard_map/ppermute | solution.py:23
  260.3 13.5 %collective-permute-start.36 = (bf16[1,80,128]{2,1,0:T(8,128)(2,1)S(1)}, bf16[1,80,128]{2,1,0:T(8,128)(2,1)S(1)}, u32[]{:S(2)}, u32[]{:S(2)}) collective-permute-start(bf16[1,80,128]{2,1,0:T(8,128)(2,1)S(1)} %get-tuple-element.62), channel_id=1, source_target_pairs={{0,48},{2,50},{4,52},{6,54},{8,56},{10,58},{12,60},{14,62},{16,0},... | collective-permute-start | bytes 61448 | tf_op jit(solution)/shard_map/ppermute | solution.py:23
  270.2 18.3 %collective-permute-start.35 = (bf16[1,80,256]{2,1,0:T(8,128)(2,1)S(1)}, bf16[1,80,256]{2,1,0:T(8,128)(2,1)S(1)}, u32[]{:S(2)}, u32[]{:S(2)}) collective-permute-start(bf16[1,80,256]{2,1,0:T(8,128)(2,1)S(1)} %pad_maximum_fusion.16), channel_id=1, source_target_pairs={{0,16},{2,18},{4,20},{6,22},{8,24},{10,26},{12,28},{14,30},{16,32}... | collective-permute-start | bytes 122888 | tf_op jit(solution)/shard_map/ppermute | solution.py:23
  276.5 13.1 %collective-permute-start.37 = (bf16[1,80,256]{2,1,0:T(8,128)(2,1)S(1)}, bf16[1,80,256]{2,1,0:T(8,128)(2,1)S(1)}, u32[]{:S(2)}, u32[]{:S(2)}) collective-permute-start(bf16[1,80,256]{2,1,0:T(8,128)(2,1)S(1)} %pad_maximum_fusion.17), channel_id=1, source_target_pairs={{0,48},{2,50},{4,52},{6,54},{8,56},{10,58},{12,60},{14,62},{16,0},... | collective-permute-start | bytes 122888 | tf_op jit(solution)/shard_map/ppermute | solution.py:23
  298.7 6.9 %collective-permute-start.39 = (bf16[2,8,4096]{2,1,0:T(8,128)(2,1)S(1)}, bf16[2,8,4096]{2,1,0:T(8,128)(2,1)S(1)}, u32[]{:S(2)}, u32[]{:S(2)}) collective-permute-start(bf16[2,8,4096]{2,1,0:T(8,128)(2,1)S(1)} %get-tuple-element.29), channel_id=1, source_target_pairs={{0,2},{2,4},{4,6},{6,8},{8,10},{10,12},{12,14},{14,16},{16,18},{18... | collective-permute-start | bytes 393224 | tf_op jit(solution)/shard_map/ppermute | solution.py:23
  298.8 6.9 %collective-permute-start.43 = (bf16[2,8,4096]{2,1,0:T(8,128)(2,1)S(1)}, bf16[2,8,4096]{2,1,0:T(8,128)(2,1)S(1)}, u32[]{:S(2)}, u32[]{:S(2)}) collective-permute-start(bf16[2,8,4096]{2,1,0:T(8,128)(2,1)S(1)} %get-tuple-element.31), channel_id=1, source_target_pairs={{0,62},{2,0},{4,2},{6,4},{8,6},{10,8},{12,10},{14,12},{16,14},{18,... | collective-permute-start | bytes 393224 | tf_op jit(solution)/shard_map/ppermute | solution.py:23
  305.6 8.8 %collective-permute-start.40 = (bf16[4,8,4096]{2,1,0:T(8,128)(2,1)S(1)}, bf16[4,8,4096]{2,1,0:T(8,128)(2,1)S(1)}, u32[]{:S(2)}, u32[]{:S(2)}) collective-permute-start(bf16[4,8,4096]{2,1,0:T(8,128)(2,1)S(1)} %pad_maximum_fusion.1), channel_id=1, source_target_pairs={{0,2},{2,4},{4,6},{6,8},{8,10},{10,12},{12,14},{14,16},{16,18},{18... | collective-permute-start | bytes 786440 | tf_op jit(solution)/shard_map/ppermute | solution.py:23
  305.8 8.8 %collective-permute-start.44 = (bf16[4,8,4096]{2,1,0:T(8,128)(2,1)S(1)}, bf16[4,8,4096]{2,1,0:T(8,128)(2,1)S(1)}, u32[]{:S(2)}, u32[]{:S(2)}) collective-permute-start(bf16[4,8,4096]{2,1,0:T(8,128)(2,1)S(1)} %pad_maximum_fusion.2), channel_id=1, source_target_pairs={{0,62},{2,0},{4,2},{6,4},{8,6},{10,8},{12,10},{14,12},{16,14},{18,... | collective-permute-start | bytes 786440 | tf_op jit(solution)/shard_map/ppermute | solution.py:23
  314.5 8.0 %collective-permute-start.41 = (bf16[4,8,4096]{2,1,0:T(8,128)(2,1)S(1)}, bf16[4,8,4096]{2,1,0:T(8,128)(2,1)S(1)}, u32[]{:S(2)}, u32[]{:S(2)}) collective-permute-start(bf16[4,8,4096]{2,1,0:T(8,128)(2,1)S(1)} %fusion.35), channel_id=1, source_target_pairs={{0,2},{2,4},{4,6},{6,8},{8,10},{10,12},{12,14},{14,16},{16,18},{18... | collective-permute-start | bytes 786440 | tf_op jit(solution)/shard_map/ppermute | solution.py:23
  322.6 7.3 %collective-permute-start.45 = (bf16[4,8,4096]{2,1,0:T(8,128)(2,1)S(1)}, bf16[4,8,4096]{2,1,0:T(8,128)(2,1)S(1)}, u32[]{:S(2)}, u32[]{:S(2)}) collective-permute-start(bf16[4,8,4096]{2,1,0:T(8,128)(2,1)S(1)} %get-tuple-element.24), channel_id=1, source_target_pairs={{0,62},{2,0},{4,2},{6,4},{8,6},{10,8},{12,10},{14,12},{16,14},{18,... | collective-permute-start | bytes 786440 | tf_op jit(solution)/shard_map/ppermute | solution.py:23
  322.7 7.8 %collective-permute-start.42 = (bf16[4,8,4096]{2,1,0:T(8,128)(2,1)S(1)}, bf16[4,8,4096]{2,1,0:T(8,128)(2,1)S(1)}, u32[]{:S(2)}, u32[]{:S(2)}) collective-permute-start(bf16[4,8,4096]{2,1,0:T(8,128)(2,1)S(1)} %get-tuple-element.23), channel_id=1, source_target_pairs={{0,2},{2,4},{4,6},{6,8},{8,10},{10,12},{12,14},{14,16},{16,18},{18... | collective-permute-start | bytes 786440 | tf_op jit(solution)/shard_map/ppermute | solution.py:23
  336.6 13.6 %collective-permute-start.47 = (bf16[1,8,2048]{2,1,0:T(8,128)(2,1)S(1)}, bf16[1,8,2048]{2,1,0:T(8,128)(2,1)S(1)}, u32[]{:S(2)}, u32[]{:S(2)}) collective-permute-start(bf16[1,8,2048]{2,1,0:T(8,128)(2,1)S(1)} %get-tuple-element.55), channel_id=1, source_target_pairs={{0,16},{2,18},{4,20},{6,22},{8,24},{10,26},{12,28},{14,30},{16,32}... | collective-permute-start | bytes 98312 | tf_op jit(solution)/shard_map/ppermute | solution.py:23
  344.6 13.0 %collective-permute-start.49 = (bf16[1,8,2048]{2,1,0:T(8,128)(2,1)S(1)}, bf16[1,8,2048]{2,1,0:T(8,128)(2,1)S(1)}, u32[]{:S(2)}, u32[]{:S(2)}) collective-permute-start(bf16[1,8,2048]{2,1,0:T(8,128)(2,1)S(1)} %get-tuple-element.56), channel_id=1, source_target_pairs={{0,48},{2,50},{4,52},{6,54},{8,56},{10,58},{12,60},{14,62},{16,0},... | collective-permute-start | bytes 98312 | tf_op jit(solution)/shard_map/ppermute | solution.py:23
  357.7 16.0 %collective-permute-start.50 = (bf16[1,8,4096]{2,1,0:T(8,128)(2,1)S(1)}, bf16[1,8,4096]{2,1,0:T(8,128)(2,1)S(1)}, u32[]{:S(2)}, u32[]{:S(2)}) collective-permute-start(bf16[1,8,4096]{2,1,0:T(8,128)(2,1)S(1)} %pad_maximum_fusion.13), channel_id=1, source_target_pairs={{0,48},{2,50},{4,52},{6,54},{8,56},{10,58},{12,60},{14,62},{16,0},... | collective-permute-start | bytes 196616 | tf_op jit(solution)/shard_map/ppermute | solution.py:23
  360.3 14.7 %collective-permute-start.48 = (bf16[1,8,4096]{2,1,0:T(8,128)(2,1)S(1)}, bf16[1,8,4096]{2,1,0:T(8,128)(2,1)S(1)}, u32[]{:S(2)}, u32[]{:S(2)}) collective-permute-start(bf16[1,8,4096]{2,1,0:T(8,128)(2,1)S(1)} %pad_maximum_fusion.12), channel_id=1, source_target_pairs={{0,16},{2,18},{4,20},{6,22},{8,24},{10,26},{12,28},{14,30},{16,32}... | collective-permute-start | bytes 196616 | tf_op jit(solution)/shard_map/ppermute | solution.py:23
  375.3 13.4 %collective-permute-start.53 = (bf16[8,4096]{1,0:T(8,128)(2,1)S(1)}, bf16[8,4096]{1,0:T(8,128)(2,1)S(1)}, u32[]{:S(2)}, u32[]{:S(2)}) collective-permute-start(bf16[8,4096]{1,0:T(8,128)(2,1)S(1)} %get-tuple-element.8), channel_id=1, source_target_pairs={{0,16},{2,18},{4,20},{6,22},{8,24},{10,26},{12,28},{14,30},{16,32}... | collective-permute-start | bytes 196616 | tf_op jit(solution)/shard_map/ppermute | solution.py:23
  383.8 13.0 %collective-permute-start.51 = (bf16[8,4096]{1,0:T(8,128)(2,1)S(1)}, bf16[8,4096]{1,0:T(8,128)(2,1)S(1)}, u32[]{:S(2)}, u32[]{:S(2)}) collective-permute-start(bf16[8,4096]{1,0:T(8,128)(2,1)S(1)} %get-tuple-element.8), channel_id=1, source_target_pairs={{0,48},{2,50},{4,52},{6,54},{8,56},{10,58},{12,60},{14,62},{16,0},... | collective-permute-start | bytes 196616 | tf_op jit(solution)/shard_map/ppermute | solution.py:23
  388.7 12.6 %collective-permute-start.54 = (bf16[8,2048]{1,0:T(8,128)(2,1)S(1)}, bf16[8,2048]{1,0:T(8,128)(2,1)S(1)}, u32[]{:S(2)}, u32[]{:S(2)}) collective-permute-start(bf16[8,2048]{1,0:T(8,128)(2,1)S(1)} %slice.554), channel_id=1, source_target_pairs={{0,16},{2,18},{4,20},{6,22},{8,24},{10,26},{12,28},{14,30},{16,32}... | collective-permute-start | bytes 98312 | tf_op jit(solution)/shard_map/ppermute | solution.py:23
  396.8 13.6 %collective-permute-start.52 = (bf16[8,2048]{1,0:T(8,128)(2,1)S(1)}, bf16[8,2048]{1,0:T(8,128)(2,1)S(1)}, u32[]{:S(2)}, u32[]{:S(2)}) collective-permute-start(bf16[8,2048]{1,0:T(8,128)(2,1)S(1)} %slice.553), channel_id=1, source_target_pairs={{0,48},{2,50},{4,52},{6,54},{8,56},{10,58},{12,60},{14,62},{16,0},... | collective-permute-start | bytes 98312 | tf_op jit(solution)/shard_map/ppermute | solution.py:23
  410.5 13.4 %collective-permute-start.59 = (bf16[4,8,4096]{2,1,0:T(8,128)(2,1)S(1)}, bf16[4,8,4096]{2,1,0:T(8,128)(2,1)S(1)}, u32[]{:S(2)}, u32[]{:S(2)}) collective-permute-start(bf16[4,8,4096]{2,1,0:T(8,128)(2,1)S(1)} %pad_maximum_fusion.3), channel_id=1, source_target_pairs={{0,2},{2,4},{4,6},{6,8},{8,10},{10,12},{12,14},{14,16},{16,18},{18... | collective-permute-start | bytes 786440 | tf_op jit(solution)/shard_map/ppermute | solution.py:23
  415.0 8.9 %collective-permute-start.55 = (bf16[4,8,4096]{2,1,0:T(8,128)(2,1)S(1)}, bf16[4,8,4096]{2,1,0:T(8,128)(2,1)S(1)}, u32[]{:S(2)}, u32[]{:S(2)}) collective-permute-start(bf16[4,8,4096]{2,1,0:T(8,128)(2,1)S(1)} %pad_maximum_fusion.3), channel_id=1, source_target_pairs={{0,62},{2,0},{4,2},{6,4},{8,6},{10,8},{12,10},{14,12},{16,14},{18,... | collective-permute-start | bytes 786440 | tf_op jit(solution)/shard_map/ppermute | solution.py:23
  423.9 9.0 %collective-permute-start.60 = (bf16[4,8,4096]{2,1,0:T(8,128)(2,1)S(1)}, bf16[4,8,4096]{2,1,0:T(8,128)(2,1)S(1)}, u32[]{:S(2)}, u32[]{:S(2)}) collective-permute-start(bf16[4,8,4096]{2,1,0:T(8,128)(2,1)S(1)} %collective-permute-done.59), channel_id=1, source_target_pairs={{0,2},{2,4},{4,6},{6,8},{8,10},{10,12},{12,14},{14,16},{16,18},{18... | collective-permute-start | bytes 786440 | tf_op jit(solution)/shard_map/ppermute | solution.py:23
  423.9 9.0 %collective-permute-start.56 = (bf16[4,8,4096]{2,1,0:T(8,128)(2,1)S(1)}, bf16[4,8,4096]{2,1,0:T(8,128)(2,1)S(1)}, u32[]{:S(2)}, u32[]{:S(2)}) collective-permute-start(bf16[4,8,4096]{2,1,0:T(8,128)(2,1)S(1)} %collective-permute-done.55), channel_id=1, source_target_pairs={{0,62},{2,0},{4,2},{6,4},{8,6},{10,8},{12,10},{14,12},{16,14},{18,... | collective-permute-start | bytes 786440 | tf_op jit(solution)/shard_map/ppermute | solution.py:23
  432.8 7.6 %collective-permute-start.61 = (bf16[4,8,4096]{2,1,0:T(8,128)(2,1)S(1)}, bf16[4,8,4096]{2,1,0:T(8,128)(2,1)S(1)}, u32[]{:S(2)}, u32[]{:S(2)}) collective-permute-start(bf16[4,8,4096]{2,1,0:T(8,128)(2,1)S(1)} %collective-permute-done.60), channel_id=1, source_target_pairs={{0,2},{2,4},{4,6},{6,8},{8,10},{10,12},{12,14},{14,16},{16,18},{18... | collective-permute-start | bytes 786440 | tf_op jit(solution)/shard_map/ppermute | solution.py:23
  432.8 7.8 %collective-permute-start.57 = (bf16[4,8,4096]{2,1,0:T(8,128)(2,1)S(1)}, bf16[4,8,4096]{2,1,0:T(8,128)(2,1)S(1)}, u32[]{:S(2)}, u32[]{:S(2)}) collective-permute-start(bf16[4,8,4096]{2,1,0:T(8,128)(2,1)S(1)} %collective-permute-done.56), channel_id=1, source_target_pairs={{0,62},{2,0},{4,2},{6,4},{8,6},{10,8},{12,10},{14,12},{16,14},{18,... | collective-permute-start | bytes 786440 | tf_op jit(solution)/shard_map/ppermute | solution.py:23
  473.3 7.3 %collective-permute-start.65 = (bf16[2,8,4096]{2,1,0:T(8,128)(2,1)S(1)}, bf16[2,8,4096]{2,1,0:T(8,128)(2,1)S(1)}, u32[]{:S(2)}, u32[]{:S(2)}) collective-permute-start(bf16[2,8,4096]{2,1,0:T(8,128)(2,1)S(1)} %get-tuple-element.25), channel_id=1, source_target_pairs={{0,2},{2,4},{4,6},{6,8},{8,10},{10,12},{12,14},{14,16},{16,18},{18... | collective-permute-start | bytes 393224 | tf_op jit(solution)/shard_map/ppermute | solution.py:23
  473.4 8.3 %collective-permute-start.69 = (bf16[2,8,4096]{2,1,0:T(8,128)(2,1)S(1)}, bf16[2,8,4096]{2,1,0:T(8,128)(2,1)S(1)}, u32[]{:S(2)}, u32[]{:S(2)}) collective-permute-start(bf16[2,8,4096]{2,1,0:T(8,128)(2,1)S(1)} %get-tuple-element.27), channel_id=1, source_target_pairs={{0,62},{2,0},{4,2},{6,4},{8,6},{10,8},{12,10},{14,12},{16,14},{18,... | collective-permute-start | bytes 393224 | tf_op jit(solution)/shard_map/ppermute | solution.py:23
  481.6 9.1 %collective-permute-start.66 = (bf16[4,8,4096]{2,1,0:T(8,128)(2,1)S(1)}, bf16[4,8,4096]{2,1,0:T(8,128)(2,1)S(1)}, u32[]{:S(2)}, u32[]{:S(2)}) collective-permute-start(bf16[4,8,4096]{2,1,0:T(8,128)(2,1)S(1)} %pad_maximum_fusion.4), channel_id=1, source_target_pairs={{0,2},{2,4},{4,6},{6,8},{8,10},{10,12},{12,14},{14,16},{16,18},{18... | collective-permute-start | bytes 786440 | tf_op jit(solution)/shard_map/ppermute | solution.py:23
  482.8 9.1 %collective-permute-start.70 = (bf16[4,8,4096]{2,1,0:T(8,128)(2,1)S(1)}, bf16[4,8,4096]{2,1,0:T(8,128)(2,1)S(1)}, u32[]{:S(2)}, u32[]{:S(2)}) collective-permute-start(bf16[4,8,4096]{2,1,0:T(8,128)(2,1)S(1)} %pad_maximum_fusion.5), channel_id=1, source_target_pairs={{0,62},{2,0},{4,2},{6,4},{8,6},{10,8},{12,10},{14,12},{16,14},{18,... | collective-permute-start | bytes 786440 | tf_op jit(solution)/shard_map/ppermute | solution.py:23
  491.8 8.2 %collective-permute-start.67 = (bf16[4,8,4096]{2,1,0:T(8,128)(2,1)S(1)}, bf16[4,8,4096]{2,1,0:T(8,128)(2,1)S(1)}, u32[]{:S(2)}, u32[]{:S(2)}) collective-permute-start(bf16[4,8,4096]{2,1,0:T(8,128)(2,1)S(1)} %fusion.26), channel_id=1, source_target_pairs={{0,2},{2,4},{4,6},{6,8},{8,10},{10,12},{12,14},{14,16},{16,18},{18... | collective-permute-start | bytes 786440 | tf_op jit(solution)/shard_map/ppermute | solution.py:23
  500.2 6.8 %collective-permute-start.71 = (bf16[4,8,4096]{2,1,0:T(8,128)(2,1)S(1)}, bf16[4,8,4096]{2,1,0:T(8,128)(2,1)S(1)}, u32[]{:S(2)}, u32[]{:S(2)}) collective-permute-start(bf16[4,8,4096]{2,1,0:T(8,128)(2,1)S(1)} %get-tuple-element.22), channel_id=1, source_target_pairs={{0,62},{2,0},{4,2},{6,4},{8,6},{10,8},{12,10},{14,12},{16,14},{18,... | collective-permute-start | bytes 786440 | tf_op jit(solution)/shard_map/ppermute | solution.py:23
  500.3 8.0 %collective-permute-start.68 = (bf16[4,8,4096]{2,1,0:T(8,128)(2,1)S(1)}, bf16[4,8,4096]{2,1,0:T(8,128)(2,1)S(1)}, u32[]{:S(2)}, u32[]{:S(2)}) collective-permute-start(bf16[4,8,4096]{2,1,0:T(8,128)(2,1)S(1)} %get-tuple-element.21), channel_id=1, source_target_pairs={{0,2},{2,4},{4,6},{6,8},{8,10},{10,12},{12,14},{14,16},{16,18},{18... | collective-permute-start | bytes 786440 | tf_op jit(solution)/shard_map/ppermute | solution.py:23
  507.0 6.7 %collective-permute-start.72 = (bf16[4,8,4096]{2,1,0:T(8,128)(2,1)S(1)}, bf16[4,8,4096]{2,1,0:T(8,128)(2,1)S(1)}, u32[]{:S(2)}, u32[]{:S(2)}) collective-permute-start(bf16[4,8,4096]{2,1,0:T(8,128)(2,1)S(1)} %fusion.24), channel_id=1, source_target_pairs={{0,62},{2,0},{4,2},{6,4},{8,6},{10,8},{12,10},{14,12},{16,14},{18,... | collective-permute-start | bytes 786440 | tf_op jit(solution)/shard_map/ppermute | solution.py:23
  513.8 13.6 %collective-permute-start.73 = (bf16[1,8,2048]{2,1,0:T(8,128)(2,1)S(1)}, bf16[1,8,2048]{2,1,0:T(8,128)(2,1)S(1)}, u32[]{:S(2)}, u32[]{:S(2)}) collective-permute-start(bf16[1,8,2048]{2,1,0:T(8,128)(2,1)S(1)} %get-tuple-element.49), channel_id=1, source_target_pairs={{0,16},{2,18},{4,20},{6,22},{8,24},{10,26},{12,28},{14,30},{16,32}... | collective-permute-start | bytes 98312 | tf_op jit(solution)/shard_map/ppermute | solution.py:23
  523.5 12.6 %collective-permute-start.75 = (bf16[1,8,2048]{2,1,0:T(8,128)(2,1)S(1)}, bf16[1,8,2048]{2,1,0:T(8,128)(2,1)S(1)}, u32[]{:S(2)}, u32[]{:S(2)}) collective-permute-start(bf16[1,8,2048]{2,1,0:T(8,128)(2,1)S(1)} %get-tuple-element.50), channel_id=1, source_target_pairs={{0,48},{2,50},{4,52},{6,54},{8,56},{10,58},{12,60},{14,62},{16,0},... | collective-permute-start | bytes 98312 | tf_op jit(solution)/shard_map/ppermute | solution.py:23
  536.1 15.2 %collective-permute-start.76 = (bf16[1,8,4096]{2,1,0:T(8,128)(2,1)S(1)}, bf16[1,8,4096]{2,1,0:T(8,128)(2,1)S(1)}, u32[]{:S(2)}, u32[]{:S(2)}) collective-permute-start(bf16[1,8,4096]{2,1,0:T(8,128)(2,1)S(1)} %pad_maximum_fusion.15), channel_id=1, source_target_pairs={{0,48},{2,50},{4,52},{6,54},{8,56},{10,58},{12,60},{14,62},{16,0},... | collective-permute-start | bytes 196616 | tf_op jit(solution)/shard_map/ppermute | solution.py:23
  537.5 16.5 %collective-permute-start.74 = (bf16[1,8,4096]{2,1,0:T(8,128)(2,1)S(1)}, bf16[1,8,4096]{2,1,0:T(8,128)(2,1)S(1)}, u32[]{:S(2)}, u32[]{:S(2)}) collective-permute-start(bf16[1,8,4096]{2,1,0:T(8,128)(2,1)S(1)} %pad_maximum_fusion.14), channel_id=1, source_target_pairs={{0,16},{2,18},{4,20},{6,22},{8,24},{10,26},{12,28},{14,30},{16,32}... | collective-permute-start | bytes 196616 | tf_op jit(solution)/shard_map/ppermute | solution.py:23
  (36 other events, 745.9 us)
